TPU v7x, 32 devices: a whole 2x2x4 slice. The times are simulated.
32 devices in a mesh: freq: 16 (over z, y, x), slab: 2 (over core).
Axes of the slice: x: 2, y: 2, z: 4, core: 2. Of those that a mesh axis runs over, the one named last changes fastest.
Arguments:
- log_conductivity: float32 [10, 32, 128], P('slab'), may hold values from -1 to 1
- omega: float32 [16], P('freq'), may hold values from 0.1 to 2
- sources: float32 [16, 2, 2, 3, 10, 32, 128], P('freq', None, None, None, 'slab'), may hold values from -8 to 8
- receivers: int32 [256], P('slab'), may hold values from 0 to 20479
- observed: float32 [16, 2, 2, 3, 256], P('freq', None, None, None, 'slab'), may hold values from -2.4 to 2.4
- data_weight: float32 [16, 2, 3, 256], P('freq', None, None, 'slab'), may hold values from 3 to 30
- prior_gradient: float32 [10, 32, 128], P('slab', 'freq'), may hold values from -6 to 6
- prior_direction: float32 [10, 32, 128], P('slab', 'freq'), may hold values from -6 to 6
- step_length: float32 [1], replicated, may hold values from 0.2 to 0.6
Outputs:
- unit_direction: float32 [10, 32, 128], P('slab', 'freq')
- trial_model: float32 [10, 32, 128], P('slab')
Inputs may be any that keep to these rules, and one draw needn't show every extreme that they name: Each block of 128 receivers belongs to one slab of 5 layers, slabs in order; an entry is z * 32 * 128 + y * 128 + x within its slab; cells may repeat.
All inputs are finite; a program needn't handle non-finite values.
Results may differ from a plain program's by a relative error of at most 0.0011.
Values sent between devices are 32-bit elements; how exact they have to be, the bound alone decides.
A program may use at most 128 MiB of HBM per device.

v0:
```python
import jax
import jax.numpy as jnp
from jax import lax
from jax.sharding import PartitionSpec as P

ITERS = 4


epsilon = 1e-06


def padded_2(shard, sides, width):
    for axis, dim in sides:
        size, length = (lax.axis_size(axis), shard.shape[dim])
        up = [(i, (i + 1) % size) for i in range(size - 1)]
        down = [(j, i) for i, j in up]
        last = lax.slice_in_dim(shard, length - width, length, axis=dim)
        leading = lax.slice_in_dim(shard, 0, width, axis=dim)
        before = lax.ppermute(last, axis, up)
        after = lax.ppermute(leading, axis, down)
        shard = jnp.concatenate([before, shard, after], axis=dim)
    return shard


def complex_div(dividend, divisor):
    modulus = divisor[0] * divisor[0] + divisor[1] * divisor[1]
    return jnp.stack(
        [
            (dividend[0] * divisor[0] + dividend[1] * divisor[1]) / modulus,
            (dividend[1] * divisor[0] - dividend[0] * divisor[1]) / modulus,
        ]
    )


def scaled(factor, vector):
    factor_re = factor[0][:, None, None, None, None]
    factor_im = factor[1][:, None, None, None, None]
    return jnp.stack(
        [
            factor_re * vector[:, 0] - factor_im * vector[:, 1],
            factor_re * vector[:, 1] + factor_im * vector[:, 0],
        ],
        axis=1,
    )


def inner_sums(former, latter):
    real_part = jnp.sum(
        former[:, 0] * latter[:, 0] - former[:, 1] * latter[:, 1], axis=(1, 2, 3, 4)
    )
    imag_part = jnp.sum(
        former[:, 0] * latter[:, 1] + former[:, 1] * latter[:, 0], axis=(1, 2, 3, 4)
    )
    return jnp.stack([real_part, imag_part])


def operate(electric, coupling):
    padded = padded_2(electric, (("slab", 3),), 1)
    padded = jnp.pad(padded, ((0, 0), (0, 0), (0, 0), (0, 0), (1, 1), (1, 1)))
    beside = padded[..., 2:, 1:-1, 1:-1] + padded[..., :-2, 1:-1, 1:-1]
    beside = beside + padded[..., 1:-1, 2:, 1:-1] + padded[..., 1:-1, :-2, 1:-1]
    beside = beside + padded[..., 1:-1, 1:-1, 2:] + padded[..., 1:-1, 1:-1, :-2]
    laplace = 6.0 * electric - beside
    return jnp.stack(
        [laplace[:, 0] - coupling * electric[:, 1], laplace[:, 1] + coupling * electric[:, 0]],
        axis=1,
    )


def norm_total(residual):
    return lax.psum(inner_sums(residual, residual), "slab")


def krylov_solve(source, coupling):
    solution = jnp.zeros_like(source)
    residual = source
    direction = source
    rho_now = norm_total(residual)
    for iteration in range(ITERS):
        image = operate(direction, coupling)
        curvature = lax.psum(inner_sums(direction, image), "slab")
        alpha_step = complex_div(rho_now, curvature)
        solution = solution + scaled(alpha_step, direction)
        residual = residual - scaled(alpha_step, image)
        if iteration + 1 < ITERS:
            rho_next = norm_total(residual)
            beta_ratio = complex_div(rho_next, rho_now)
            direction = residual + scaled(beta_ratio, direction)
            rho_now = rho_next
    return solution


def new_direction(gradient, prior_dir, grad_sq, grad_prior, prior_sq, total_cells):
    mean_square = grad_sq / total_cells
    root_mean = jnp.sqrt(mean_square + epsilon)
    scaled_grad = gradient / root_mean
    beta_ratio = (grad_sq / (mean_square + epsilon) - grad_prior / root_mean) / (prior_sq + epsilon)
    return -scaled_grad + beta_ratio * prior_dir


def per_device(
    log_conductivity,
    omega,
    sources,
    receivers,
    observed,
    data_weight,
    prior_gradient,
    prior_direction,
    step_length,
):
    prior_whole, direction_whole = (
        lax.all_gather(prior_gradient, "freq", axis=1, tiled=True),
        lax.all_gather(prior_direction, "freq", axis=1, tiled=True),
    )
    conductivity = jnp.exp(log_conductivity)
    coupling = omega[0] * conductivity
    electric = krylov_solve(sources[0], coupling)
    flat_field = electric.reshape(2, 2, 3, -1)
    misfit = flat_field[..., receivers] - observed[0]
    weight_sq = data_weight[0] * data_weight[0]
    adjoint_data = jnp.stack([weight_sq * misfit[:, 0], -weight_sq * misfit[:, 1]], axis=1)
    adjoint_source = (
        jnp.zeros_like(flat_field).at[..., receivers].add(adjoint_data).reshape(electric.shape)
    )
    adjoint = krylov_solve(adjoint_source, coupling)
    local_term = coupling * jnp.sum(
        adjoint[:, 0] * electric[:, 1] + adjoint[:, 1] * electric[:, 0], axis=(0, 1)
    )
    total_cells = local_term.size * lax.axis_size("slab")
    gradient = lax.psum(local_term, "freq")
    grad_sq, grad_prior, prior_sq = lax.psum(
        (
            jnp.sum(gradient * gradient),
            jnp.sum(gradient * prior_whole),
            jnp.sum(prior_whole * prior_whole),
        ),
        "slab",
    )
    direction = new_direction(gradient, direction_whole, grad_sq, grad_prior, prior_sq, total_cells)
    dir_total = lax.psum(jnp.sum(direction * direction), "slab")
    unit_whole = direction / jnp.sqrt(dir_total / total_cells + epsilon)
    own_rows = prior_gradient.shape[1]
    unit_dir = lax.dynamic_slice_in_dim(unit_whole, lax.axis_index("freq") * own_rows, own_rows, 1)
    trial_model = log_conductivity + step_length[0] * unit_whole
    return (unit_dir, trial_model)


def solution(mesh):
    in_specs = (
        P("slab", None, None),
        P("freq"),
        P("freq", None, None, None, "slab", None, None),
        P("slab"),
        P("freq", None, None, None, "slab"),
        P("freq", None, None, "slab"),
        P("slab", "freq", None),
        P("slab", "freq", None),
        P(),
    )
    out_specs = (P("slab", "freq", None), P("slab", None, None))
    return jax.shard_map(
        per_device, mesh=mesh, in_specs=in_specs, out_specs=out_specs, check_vma=False
    )
```

profile of v0, /device:TPU:0, one launch (start us, length us, event | category | flops | bytes accessed | tf_op | source)
XLA Modules:
  0.0 447.4 jit_solution(8006285140482710032)
XLA Ops:
  17.9 3.3 all-reduce.10
  22.9 2.5 psum.149
  34.3 2.5 psum.150
  38.6 2.5 psum.151
  49.8 2.5 psum.152
  54.1 2.5 psum.153
  65.4 2.6 psum.154
  69.1 4.1 fusion.20
  73.3 36.0 %copy.232 = f32[2,2,3,20480]{2,1,3,0:T(2,128)} copy(f32[2,2,3,20480]{3,1,2,0:T(2,128)S(1)} %fusion.20) | data formatting | bytes 1966080 | tf_op jit(solution)/shard_map/add | solution.py:83
  111.7 13.5 %broadcast_in_dim.4 = f32[2,2,3,20480]{2,1,3,0:T(2,128)} broadcast(f32[]{:T(128)} %constant.10.clone.1), dimensions={} | broadcast | bytes 983044 | tf_op jit(solution)/shard_map/broadcast_in_dim | solution.py:124
  125.2 13.3 %scatter_fusion = f32[2,2,3,20480]{2,1,3,0:T(2,128)} fusion(f32[2,2,3,20480]{2,1,3,0:T(2,128)} %broadcast_in_dim.4, s32[128]{0:T(128)S(1)} %compare_select_fusion, f32[128,2,2,3]{3,2,1,0:T(2,128)S(1)} %copy.237), kind=kCustom, calls=%fused_computation.1 | custom fusion | flops 1536 | bytes 18944 | tf_op jit(solution)/shard_map/scatter-add | solution.py:124
  138.5 33.1 %copy.238 = f32[2,2,3,5,32,128]{5,4,3,2,0,1:T(8,128)S(1)} copy(f32[2,2,3,5,32,128]{2,1,5,4,3,0:T(2,128)} %bitcast.561) | data formatting | bytes 1966080 | tf_op jit(solution)/shard_map/reshape | solution.py:124
  180.1 2.5 all-reduce.9
  184.5 2.5 psum.157
  199.2 2.5 multiply_subtract_fusion.7
  203.1 2.5 psum.159
  219.1 2.5 multiply_subtract_fusion.3
  222.6 2.5 psum.161
  231.4 44.8 %all_gather.6 = f32[5,32,128]{2,0,1:T(8,128)} all-gather(f32[5,2,128]{2,0,1:T(8,128)S(1)} %copy.252), channel_id=1, replica_groups=mesh['freq'=16,'slab'=2] {'freq'}, dimensions={1}, use_global_device_ids=true | all-gather | bytes 87040 | tf_op jit(solution)/shard_map/all_gather | solution.py:113
  276.2 38.5 %all_gather.7 = f32[5,32,128]{2,0,1:T(8,128)} all-gather(f32[5,2,128]{2,0,1:T(8,128)S(1)} %copy.254), channel_id=1, replica_groups=mesh['freq'=16,'slab'=2] {'freq'}, dimensions={1}, use_global_device_ids=true | all-gather | bytes 87040 | tf_op jit(solution)/shard_map/all_gather | solution.py:114
  318.7 2.5 psum.162
  324.9 101.7 %all-reduce.13.cloned.1.call-done = f32[5,32,128]{2,1,0:T(8,128)} async-done(((f32[5,32,128]{2,1,0:T(8,128)}), f32[5,32,128]{2,1,0:T(8,128)}) %all-reduce.13.cloned.1.call-update) | async-done | bytes 81936 | tf_op jit(solution)/shard_map/psum | solution.py:131
  428.1 3.1 all-reduce.8
  435.5 3.1 psum.167
  (218 shorter events, 100.9 us)
Async XLA Ops:
  7.2 7.8 %copy-start = (f32[1,2,2,3,5,32,128]{6,5,4,3,2,1,0:T(8,128)S(1)}, f32[1,2,2,3,5,32,128]{6,5,4,3,2,1,0:T(8,128)}, u32[]{:S(2)}) copy-start(f32[1,2,2,3,5,32,128]{6,5,4,3,2,1,0:T(8,128)} %param.11) | copy-start | bytes 2949124
  7.2 419.4 %all-reduce.13.cloned.1.call-start = ((), (), s32[]{:S(2)}) async-start(), calls=%async_computation | async-start | bytes 163840 | tf_op jit(solution)/shard_map/psum | solution.py:131
  8.4 6.5 %collective-permute-start.1 = (f32[2,2,3,1,32,128]{5,4,3,2,0,1:T(8,128)S(1)}, f32[2,2,3,1,32,128]{5,4,3,2,0,1:T(8,128)S(1)}, u32[]{:S(2)}, u32[]{:S(2)}) collective-permute-start(f32[2,2,3,1,32,128]{5,4,3,2,0,1:T(8,128)S(1)} %get-tuple-element.109), channel_id=1, source_target_pairs={{0,1},{2,3},{4,5},{6,7},{8,9},{10,11},{12,13},{14,15},{16,17},{18,... | collective-permute-start | bytes 589832 | tf_op jit(solution)/shard_map/ppermute | solution.py:19
  10.8 4.1 collective-permute-start
  22.4 45.9 %copy-start.5 = (f32[2,1,3,5,32,128]{5,4,3,2,0,1:T(8,128)}, f32[2,1,3,5,32,128]{5,4,3,2,0,1:T(8,128)S(1)}, u32[]{:S(2)}) copy-start(f32[2,1,3,5,32,128]{5,4,3,2,0,1:T(8,128)S(1)} %get-tuple-element.87) | copy-start | bytes 1474564
  25.8 3.6 collective-permute-start.3
  28.1 3.3 collective-permute-start.2
  41.5 3.4 collective-permute-start.5
  43.6 3.3 collective-permute-start.4
  53.8 6.8 %copy-start.32 = (s32[128]{0:T(128)S(1)}, s32[128]{0:T(128)}, u32[]{:S(2)}) copy-start(s32[128]{0:T(128)} %param.12) | copy-start | bytes 1540
  57.0 3.7 collective-permute-start.7
  59.1 3.3 collective-permute-start.6
  73.2 38.2 %copy-start.28 = (f32[1,2,2,3,128]{4,2,3,1,0:T(2,128)S(1)}, f32[1,2,2,3,128]{4,2,3,1,0:T(2,128)}, u32[]{:S(2)}) copy-start(f32[1,2,2,3,128]{4,2,3,1,0:T(2,128)} %param.13) | copy-start | bytes 18436
  73.3 38.2 %copy-start.31 = (f32[1,2,3,128]{3,1,2,0:T(2,128)S(1)}, f32[1,2,3,128]{3,1,2,0:T(2,128)}, u32[]{:S(2)}) copy-start(f32[1,2,3,128]{3,1,2,0:T(2,128)} %param.14) | copy-start | bytes 9220
  171.6 3.4 collective-permute-start.9
  173.7 3.3 collective-permute-start.8
  187.5 3.6 collective-permute-start.11
  189.6 3.3 collective-permute-start.10
  207.3 3.4 collective-permute-start.13
  209.4 3.3 collective-permute-start.12
  225.4 6.0 %copy-start.30 = (f32[5,2,128]{2,1,0:T(2,128)S(1)}, f32[5,2,128]{2,1,0:T(2,128)}, u32[]{:S(2)}) copy-start(f32[5,2,128]{2,1,0:T(2,128)} %param.16) | copy-start | bytes 15364
  227.3 87.3 %collective-permute-start.15 = (f32[2,2,3,1,32,128]{5,4,3,2,0,1:T(8,128)S(1)}, f32[2,2,3,1,32,128]{5,4,3,2,0,1:T(8,128)S(1)}, u32[]{:S(2)}, u32[]{:S(2)}) collective-permute-start(f32[2,2,3,1,32,128]{5,4,3,2,0,1:T(8,128)S(1)} %get-tuple-element.95), channel_id=1, source_target_pairs={{0,1},{2,3},{4,5},{6,7},{8,9},{10,11},{12,13},{14,15},{16,17},{18,... | collective-permute-start | bytes 589832 | tf_op jit(solution)/shard_map/ppermute | solution.py:19
  229.4 85.2 %collective-permute-start.14 = (f32[2,2,3,1,32,128]{5,4,3,2,0,1:T(8,128)S(1)}, f32[2,2,3,1,32,128]{5,4,3,2,0,1:T(8,128)S(1)}, u32[]{:S(2)}, u32[]{:S(2)}) collective-permute-start(f32[2,2,3,1,32,128]{5,4,3,2,0,1:T(8,128)S(1)} %get-tuple-element.96), channel_id=1, source_target_pairs={{1,0},{3,2},{5,4},{7,6},{9,8},{11,10},{13,12},{15,14},{17,16},{19,... | collective-permute-start | bytes 589832 | tf_op jit(solution)/shard_map/ppermute | solution.py:20
  321.4 112.6 %copy-start.27 = (f32[5,32,128]{2,0,1:T(8,128)S(1)}, f32[5,32,128]{2,0,1:T(8,128)}, u32[]{:S(2)}) copy-start(f32[5,32,128]{2,0,1:T(8,128)} %all_gather.7) | copy-start | bytes 245764
  (26 other events, 58.8 us)
Sparse Core Ops, SparseCore 0:
  324.3 102.2 all-reduce.12
where the time goes:
time: 449 us; the launch traced here: 447 us
  blocking collectives  125 us (28%)
  waiting for transfers between devices  113 us (25%)
  local copies, waits for them, and re-layouts  92.7 us (21%)
  other arithmetic  68.7 us (15%)
  starting transfers between devices  28 us (6%)
  between operations  19.7 us (4%)
    psum x1, waiting for transfers between devices, per_device(): gradient = lax.psum(local_term, 'freq')  102 us
    all_gather x1, blocking collectives, per_device(): lax.all_gather(prior_gradient, 'freq', axis=1, tiled=True)  44.8 us
    all_gather x1, blocking collectives, per_device(): lax.all_gather(prior_direction, 'freq', axis=1, tiled=True)  38.5 us
    add x1, local copies, waits for them, and re-layouts, krylov_solve(): solution = solution + scaled(alpha_step, direction)  36 us
    reshape x1, local copies, waits for them, and re-layouts, per_device(): jnp.zeros_like(flat_field).at[..., receivers].add(adjoint_data)  33.1 us
    psum x8, blocking collectives, krylov_solve(): curvature = lax.psum(inner_sums(direction, image), 'slab')  20.7 us
    ppermute x8, starting transfers between devices, padded_2(): before = lax.ppermute(last, axis, up)  17.2 us
    psum x6, blocking collectives, norm_total(): return lax.psum(inner_sums(residual, residual), 'slab')  14.8 us
  transfers between devices with their start and end apart: 17, of which 7 were waited for; matrix products, arithmetic and copies ran while one was open for 1% of the time, Pallas kernels for 0%

commit v1 on v0

v1 whole, which is shorter than its diff:
```python
import functools

import jax
import jax.numpy as jnp
from jax import lax
from jax.experimental import pallas as pl
from jax.experimental.pallas import tpu as pltpu
from jax.sharding import PartitionSpec as P

ITERS = 4
PAD = 8
EPSILON = 1e-06
POLS = 2

F32 = jnp.float32


def complex_div(dividend, divisor):
    modulus = divisor[0] * divisor[0] + divisor[1] * divisor[1]
    return (
        (dividend[0] * divisor[0] + dividend[1] * divisor[1]) / modulus,
        (dividend[1] * divisor[0] - dividend[0] * divisor[1]) / modulus,
    )


def whole_sum(part):
    return jnp.sum(jnp.sum(part, axis=0, keepdims=True), axis=1, keepdims=True)


def fold(plane):
    return jnp.sum(plane.reshape(-1, 8, plane.shape[-1]), axis=0)


def three_parts(value):
    high = value.astype(jnp.bfloat16)
    rest = value - high.astype(F32)
    middle = rest.astype(jnp.bfloat16)
    low = (rest - middle.astype(F32)).astype(jnp.bfloat16)
    return high, middle, low


def selected(chooser, value):
    total = None
    for part in three_parts(value):
        product = jnp.dot(chooser, part, preferred_element_type=F32)
        total = product if total is None else total + product
    return total


def kernel(
    sizes,
    omega, step_length, sources, log_cond, receivers, observed, weights, prior_grad, prior_dir,
    unit_out, trial_out,
    residual, direction, image, field, adjoint, coupling, log_all, rec_all, obs_all, wgt_all,
    small, term, term_in, flat, outgoing, incoming, own_part, gathered, grad, pg_parts, pd_parts,
    pg_whole, pd_whole, sums_own, sums_in, unit_whole,
    local_sem, slab_send, slab_recv, freq_send, freq_recv, pair_send, pair_recv,
):
    n_freq, n_slab, comps, cz, ny, nx = sizes
    nz, rows = cz * n_slab, cz * ny
    share = rows // n_freq
    own_rows = ny // n_freq
    f, s = lax.axis_index("freq"), lax.axis_index("slab")
    pol = lax.rem(s, POLS)

    own_layers = pl.ds(s * cz, cz)
    local = [
        pltpu.make_async_copy(a, b, local_sem.at[i])
        for i, (a, b) in enumerate(
            [
                (sources.at[0, pol], residual.at[:, :, own_layers]),
                (log_cond, log_all.at[s]),
                (receivers, rec_all.at[s]),
                (observed.at[0, pol], obs_all.at[s]),
                (weights.at[0, pol], wgt_all.at[s]),
                (prior_grad, pg_parts.at[f]),
                (prior_dir, pd_parts.at[f]),
            ]
        )
    ]
    for copy in local:
        copy.start()

    barrier = pltpu.get_barrier_semaphore()

    def greet_slab(j, carry):
        pl.semaphore_signal(barrier, inc=1, device_id={"slab": lax.rem(s + j, n_slab)}, device_id_type=pl.DeviceIdType.MESH)
        return carry

    def greet_freq(k, carry):
        pl.semaphore_signal(barrier, inc=1, device_id={"freq": lax.rem(f + k, n_freq)}, device_id_type=pl.DeviceIdType.MESH)
        return carry

    lax.fori_loop(1, n_freq, greet_freq, 0)
    lax.fori_loop(1, n_slab, greet_slab, 0)

    def to_slab(i, j, source, target):
        return pltpu.make_async_remote_copy(
            src_ref=source, dst_ref=target,
            send_sem=slab_send.at[i, j], recv_sem=slab_recv.at[i, j],
            device_id={"slab": lax.rem(s + j, n_slab)}, device_id_type=pl.DeviceIdType.MESH,
        )

    def to_freq(i, k, source, target):
        return pltpu.make_async_remote_copy(
            src_ref=source, dst_ref=target,
            send_sem=freq_send.at[i, k], recv_sem=freq_recv.at[i, k],
            device_id={"freq": lax.rem(f + k, n_freq)}, device_id_type=pl.DeviceIdType.MESH,
        )

    def slab_inputs(j):
        theirs = lax.rem(lax.rem(s + j, n_slab), POLS)
        return [
            to_slab(0, j, sources.at[0, theirs], residual.at[:, :, own_layers]),
            to_slab(1, j, log_cond, log_all.at[s]),
            to_slab(2, j, receivers, rec_all.at[s]),
            to_slab(3, j, observed.at[0, theirs], obs_all.at[s]),
            to_slab(4, j, weights.at[0, theirs], wgt_all.at[s]),
        ]

    def freq_inputs(k):
        return [
            to_freq(0, k, prior_grad, pg_parts.at[f]),
            to_freq(1, k, prior_dir, pd_parts.at[f]),
        ]

    zero_plane = jnp.zeros((ny + 2 * PAD, nx), F32)
    zero_rows = jnp.zeros((PAD, nx), F32)
    for c in range(2 * comps):
        direction[c, 0] = zero_plane
        direction[c, nz + 1] = zero_plane

    def clear(z, carry):
        for c in range(2 * comps):
            direction[c, z, 0:PAD] = zero_rows
            direction[c, z, PAD + ny:] = zero_rows
        return carry

    lax.fori_loop(1, nz + 1, clear, 0)

    pl.semaphore_wait(barrier, n_freq - 1 + n_slab - 1)
    for j in range(1, n_slab):
        for copy in slab_inputs(j):
            copy.start()

    def start_freq(k, carry):
        for copy in freq_inputs(k):
            copy.start()
        return carry

    lax.fori_loop(1, n_freq, start_freq, 0)
    for copy in local:
        copy.wait()
    for j in range(1, n_slab):
        for copy in slab_inputs(j):
            copy.wait()

    def couple(t, carry):
        coupling[pl.ds(t * cz, cz)] = omega[0] * jnp.exp(log_all[t])
        return carry

    lax.fori_loop(0, n_slab, couple, 0)

    lane = lax.broadcasted_iota(jnp.int32, (ny, nx), 1)
    first, last = lane == 0, lane == nx - 1
    inner = slice(PAD, PAD + ny)
    zero_acc = jnp.zeros((8, nx), F32)

    def product_sum(acc, u, v):
        return (
            acc[0] + fold(u[0] * v[0] - u[1] * v[1]),
            acc[1] + fold(u[0] * v[1] + u[1] * v[0]),
        )

    def totals(acc):
        return whole_sum(acc[0]), whole_sum(acc[1])

    def krylov_solve(target, final):
        def begin(z, acc):
            for c in range(comps):
                b = (residual[0, c, z], residual[1, c, z])
                direction[c, z + 1, inner] = b[0]
                direction[comps + c, z + 1, inner] = b[1]
                acc = product_sum(acc, b, b)
            return acc

        rho = totals(lax.fori_loop(0, nz, begin, (zero_acc, zero_acc)))

        def operate(z, acc):
            coup = coupling[z]
            for c in range(comps):
                laplace, centre = [], []
                for r in range(2):
                    i = r * comps + c
                    d = direction[i, z + 1, inner]
                    beside = direction[i, z + 2, inner] + direction[i, z, inner]
                    beside = beside + direction[i, z + 1, PAD + 1:PAD + 1 + ny]
                    beside = beside + direction[i, z + 1, PAD - 1:PAD - 1 + ny]
                    beside = beside + jnp.where(first, 0.0, pltpu.roll(d, 1, 1))
                    beside = beside + jnp.where(last, 0.0, pltpu.roll(d, nx - 1, 1))
                    laplace.append(6.0 * d - beside)
                    centre.append(d)
                out = (laplace[0] - coup * centre[1], laplace[1] + coup * centre[0])
                image[0, c, z] = out[0]
                image[1, c, z] = out[1]
                acc = product_sum(acc, centre, out)
            return acc

        for iteration in range(ITERS):
            curvature = totals(lax.fori_loop(0, nz, operate, (zero_acc, zero_acc)))
            alpha = complex_div(rho, curvature)
            alpha = (jnp.broadcast_to(alpha[0], (ny, nx)), jnp.broadcast_to(alpha[1], (ny, nx)))
            if iteration + 1 == ITERS:
                lax.fori_loop(0, nz, functools.partial(final, alpha), 0)
                break

            def update(z, acc, alpha=alpha, iteration=iteration):
                for c in range(comps):
                    d = (direction[c, z + 1, inner], direction[comps + c, z + 1, inner])
                    m = (image[0, c, z], image[1, c, z])
                    gain = (alpha[0] * d[0] - alpha[1] * d[1], alpha[0] * d[1] + alpha[1] * d[0])
                    if iteration:
                        gain = (target[0, c, z] + gain[0], target[1, c, z] + gain[1])
                    target[0, c, z] = gain[0]
                    target[1, c, z] = gain[1]
                    left = (
                        residual[0, c, z] - (alpha[0] * m[0] - alpha[1] * m[1]),
                        residual[1, c, z] - (alpha[0] * m[1] + alpha[1] * m[0]),
                    )
                    residual[0, c, z] = left[0]
                    residual[1, c, z] = left[1]
                    acc = product_sum(acc, left, left)
                return acc

            rho_next = totals(lax.fori_loop(0, nz, update, (zero_acc, zero_acc)))
            beta = complex_div(rho_next, rho)
            beta = (jnp.broadcast_to(beta[0], (ny, nx)), jnp.broadcast_to(beta[1], (ny, nx)))
            rho = rho_next

            def turn(z, carry, beta=beta):
                for c in range(comps):
                    d = (direction[c, z + 1, inner], direction[comps + c, z + 1, inner])
                    direction[c, z + 1, inner] = residual[0, c, z] + (beta[0] * d[0] - beta[1] * d[1])
                    direction[comps + c, z + 1, inner] = residual[1, c, z] + (beta[0] * d[1] + beta[1] * d[0])
                return carry

            lax.fori_loop(0, nz, turn, 0)

    def stepped(target, alpha, z, c):
        d = (direction[c, z + 1, inner], direction[comps + c, z + 1, inner])
        return (
            target[0, c, z] + (alpha[0] * d[0] - alpha[1] * d[1]),
            target[1, c, z] + (alpha[0] * d[1] + alpha[1] * d[0]),
        )

    def keep_field(alpha, z, carry):
        for c in range(comps):
            value = stepped(field, alpha, z, c)
            field[0, c, z] = value[0]
            field[1, c, z] = value[1]
        return carry

    krylov_solve(field, keep_field)

    recs = rec_all.shape[-1]
    for t in range(n_slab):
        layers = slice(t * cz, (t + 1) * cz)
        small[0:comps] = obs_all[t, 0]
        small[comps:2 * comps] = obs_all[t, 1]
        small[2 * comps:3 * comps] = wgt_all[t]
        cell = rec_all[t]
        small[3 * comps:3 * comps + 1] = cell.astype(F32)
        columns = small[...].T
        cell_column = columns[:, 3 * comps:3 * comps + 1].astype(jnp.int32)
        row_of = (lax.broadcasted_iota(jnp.int32, (recs, rows), 1) == cell_column // nx)
        lane_of = lax.broadcasted_iota(jnp.int32, (recs, nx), 1) == lax.rem(cell_column, nx)
        row_back = lax.broadcasted_iota(jnp.int32, (rows, recs), 0) == cell // nx
        row_of = row_of.astype(F32).astype(jnp.bfloat16)
        row_back = row_back.astype(F32).astype(jnp.bfloat16)
        values = jnp.concatenate(
            [field[r, c, layers].reshape(rows, nx) for r in range(2) for c in range(comps)], axis=1
        )
        picked = selected(row_of, values)
        spread = []
        for r in range(2):
            for c in range(comps):
                i = r * comps + c
                weight = columns[:, 2 * comps + c:2 * comps + c + 1]
                misfit = picked[:, i * nx:(i + 1) * nx] - columns[:, i:i + 1]
                weight_sq = weight * weight
                spread.append(jnp.where(lane_of, (weight_sq if r == 0 else -weight_sq) * misfit, 0.0))
        back = selected(row_back, jnp.concatenate(spread, axis=1))
        for r in range(2):
            for c in range(comps):
                i = r * comps + c
                residual[r, c, layers] = back[:, i * nx:(i + 1) * nx].reshape(cz, ny, nx)

    def keep_term(alpha, z, carry):
        total = jnp.zeros((ny, nx), F32)
        for c in range(comps):
            value = stepped(adjoint, alpha, z, c)
            total = total + (value[0] * field[1, c, z] + value[1] * field[0, c, z])
        term[z] = coupling[z] * total
        return carry

    krylov_solve(adjoint, keep_term)

    partner = s + 1 - 2 * pol
    swap = pltpu.make_async_remote_copy(
        src_ref=term.at[pl.ds(partner * cz, cz)], dst_ref=term_in,
        send_sem=pair_send, recv_sem=pair_recv,
        device_id={"slab": partner}, device_id_type=pl.DeviceIdType.MESH,
    )
    swap.start()

    def wait_freq(k, carry):
        for copy in freq_inputs(k):
            copy.wait()
        return carry

    lax.fori_loop(1, n_freq, wait_freq, 0)
    swap.wait()

    flat[...] = (term[own_layers] + term_in[...]).reshape(rows, nx)
    for g in range(n_freq):
        outgoing[g] = flat[g * share:(g + 1) * share]

    def scatter(k):
        return to_freq(2, k, outgoing.at[lax.rem(f + k, n_freq)], incoming.at[k])

    def spread_out(k):
        return to_freq(3, k, own_part, gathered.at[f])

    def start_scatter(k, carry):
        scatter(k).start()
        return carry

    lax.fori_loop(1, n_freq, start_scatter, 0)
    for g in range(n_freq):
        pg_whole[:, g * own_rows:(g + 1) * own_rows] = pg_parts[g]
        pd_whole[:, g * own_rows:(g + 1) * own_rows] = pd_parts[g]

    def wait_scatter(k, carry):
        scatter(k).wait()
        return carry

    lax.fori_loop(1, n_freq, wait_scatter, 0)
    mine = outgoing[f]
    for k in range(1, n_freq):
        mine = mine + incoming[k]
    own_part[...] = mine

    def start_spread(k, carry):
        spread_out(k).start()
        return carry

    def wait_spread(k, carry):
        spread_out(k).wait()
        return carry

    lax.fori_loop(1, n_freq, start_spread, 0)
    gathered[f] = mine
    lax.fori_loop(1, n_freq, wait_spread, 0)
    for g in range(n_freq):
        grad[g * share:(g + 1) * share] = gathered[g]

    gradient = grad[...]
    prior = pg_whole[...].reshape(rows, nx)
    before = pd_whole[...].reshape(rows, nx)
    pairs = [(gradient, gradient), (gradient, prior), (prior, prior), (gradient, before), (before, before)]
    for i, (u, v) in enumerate(pairs):
        sums_own[i:i + 1] = jnp.sum(fold(u * v), axis=0, keepdims=True)
    for j in range(1, n_slab):
        to_slab(5, j, sums_own, sums_in.at[j]).start()
    for j in range(1, n_slab):
        to_slab(5, j, sums_own, sums_in.at[j]).wait()
    sums = sums_own[...]
    for j in range(1, n_slab):
        sums = sums + sums_in[j]
    sums = jnp.sum(sums, axis=1, keepdims=True)
    grad_sq, grad_prior, prior_sq, grad_dir, dir_sq = [sums[i:i + 1] for i in range(len(pairs))]
    cells = float(rows * nx * n_slab)
    mean_square = grad_sq / cells
    root_mean = jnp.sqrt(mean_square + EPSILON)
    beta_ratio = (grad_sq / (mean_square + EPSILON) - grad_prior / root_mean) / (prior_sq + EPSILON)
    total = (
        grad_sq / (mean_square + EPSILON)
        - 2.0 * beta_ratio * (grad_dir / root_mean)
        + beta_ratio * beta_ratio * dir_sq
    )
    norm = jnp.sqrt(jnp.maximum(total, 0.0) / cells + EPSILON)
    unit = (gradient * (-1.0 / (root_mean * norm)) + before * (beta_ratio / norm)).reshape(cz, ny, nx)
    trial_out[...] = log_all[s] + step_length[0] * unit
    unit_whole[...] = unit
    unit_out[...] = unit_whole[:, pl.ds(f * own_rows, own_rows), :]


def per_device(n_freq, n_slab, *args):
    (log_cond, omega, sources, receivers, observed, weights, prior_grad, prior_dir, step) = args
    cz, ny, nx = log_cond.shape
    comps = sources.shape[3]
    recs = receivers.shape[0]
    nz, rows = cz * n_slab, cz * ny
    share, own_rows = rows // n_freq, prior_grad.shape[1]
    vec = lambda *shape: pltpu.VMEM(shape, F32)
    dma = lambda *shape: pltpu.SemaphoreType.DMA(shape)
    complex_field = vec(2, comps, nz, ny, nx)
    smem = pl.BlockSpec(memory_space=pltpu.SMEM)
    anywhere = pl.BlockSpec(memory_space=pl.ANY)
    inside = pl.BlockSpec(memory_space=pltpu.VMEM)
    scratch = [
        complex_field,
        vec(2 * comps, nz + 2, ny + 2 * PAD, nx),
        complex_field,
        complex_field,
        complex_field,
        vec(nz, ny, nx),
        vec(n_slab, cz, ny, nx),
        pltpu.VMEM((n_slab, 1, recs), jnp.int32),
        vec(n_slab, 2, comps, recs),
        vec(n_slab, comps, recs),
        vec(16, recs),
        vec(nz, ny, nx),
        vec(cz, ny, nx),
        vec(rows, nx),
        vec(n_freq, share, nx),
        vec(n_freq, share, nx),
        vec(share, nx),
        vec(n_freq, share, nx),
        vec(rows, nx),
        vec(n_freq, cz, own_rows, nx),
        vec(n_freq, cz, own_rows, nx),
        vec(cz, ny, nx),
        vec(cz, ny, nx),
        vec(8, nx),
        vec(n_slab, 8, nx),
        vec(cz, ny, nx),
        dma(7),
        dma(6, n_slab),
        dma(6, n_slab),
        dma(4, n_freq),
        dma(4, n_freq),
        pltpu.SemaphoreType.DMA,
        pltpu.SemaphoreType.DMA,
    ]
    return pl.pallas_call(
        functools.partial(kernel, (n_freq, n_slab, comps, cz, ny, nx)),
        out_shape=(
            jax.ShapeDtypeStruct(prior_grad.shape, F32),
            jax.ShapeDtypeStruct(log_cond.shape, F32),
        ),
        in_specs=[smem, smem] + [anywhere] * 7,
        out_specs=(inside, inside),
        scratch_shapes=scratch,
        compiler_params=pltpu.CompilerParams(
            collective_id=0, has_side_effects=True, vmem_limit_bytes=56 * 1024 * 1024
        ),
        name="inversion",
    )(omega, step, sources, log_cond, receivers.reshape(1, recs), observed, weights, prior_grad, prior_dir)


def solution(mesh):
    in_specs = (
        P("slab", None, None),
        P("freq"),
        P("freq", None, None, None, "slab", None, None),
        P("slab"),
        P("freq", None, None, None, "slab"),
        P("freq", None, None, "slab"),
        P("slab", "freq", None),
        P("slab", "freq", None),
        P(),
    )
    out_specs = (P("slab", "freq", None), P("slab", None, None))
    body = functools.partial(per_device, mesh.shape["freq"], mesh.shape["slab"])
    return jax.shard_map(body, mesh=mesh, in_specs=in_specs, out_specs=out_specs, check_vma=False)
```

time: 449 us -> 46.5 us (0.10)
  blocking collectives: 125 us -> 0 us
  waiting for transfers between devices: 113 us -> 0 us
  local copies, waits for them, and re-layouts: 92.7 us -> 4.01 us
  other arithmetic: 68.7 us -> 0 us
  Pallas kernels: 0 us -> 40.3 us
  starting transfers between devices: 28 us -> 0 us
  between operations: 19.7 us -> 1.97 us
    psum x1 -> x0, waiting for transfers between devices: 102 us -> none  [per_device(): gradient = lax.psum(local_term, 'freq')]
    all_gather x2 -> x0, blocking collectives: 83.2 us -> none  [the longest x1 44.8 us: per_device(): lax.all_gather(prior_gradient, 'freq', axis=1, tiled=True)]
    psum x16 -> x0, blocking collectives: 41.7 us -> none  [the longest x8 20.7 us: krylov_solve(): curvature = lax.psum(inner_sums(direction, image), 'slab')]
    pallas_call x0 -> x1, Pallas kernels: none -> 40.3 us  [per_device(): pl.pallas_call(functools.partial(kernel, (n_freq, n_slab, comps, cz, ny,...]
    add x2 -> x0, local copies, waits for them, and re-layouts: 36.1 us -> none  [the longest x1 36 us: krylov_solve(): solution = solution + scaled(alpha_step, direction)]
    reshape x1 -> x0, local copies, waits for them, and re-layouts: 33.1 us -> none  [per_device(): jnp.zeros_like(flat_field).at[..., receivers].add(adjoint_data)]
    ppermute x16 -> x0, starting transfers between devices: 27.9 us -> none  [the longest x8 17.2 us: padded_2(): before = lax.ppermute(last, axis, up)]
    sub x29 -> x0, other arithmetic: 20.6 us -> none  [the longest x14 12 us: scaled(): factor_re * vector[:, 0] - factor_im * vector[:, 1]]
  transfers between devices with their start and end apart: 17 -> 0, of which waited for: 7 -> 0; matrix products, arithmetic and copies ran while one was open for 1% -> 0% of each run, Pallas kernels for 0% -> 0%
where the time goes in v1:
time: 46.5 us; the launch traced here: 46.2 us
  Pallas kernels  40.3 us (87%)
  local copies, waits for them, and re-layouts  4.01 us (9%)
  between operations  1.97 us (4%)
    pallas_call x1, Pallas kernels, per_device(): pl.pallas_call(functools.partial(kernel, (n_freq, n_slab, comps, cz, ny,...  40.3 us
    unnamed x8, local copies, waits for them, and re-layouts  4.01 us

profile of v1, /device:TPU:0, one launch (start us, length us, event | category | flops | bytes accessed | tf_op | source)
XLA Modules:
  0.0 46.2 jit_solution(14143571623495905414)
XLA Ops:
  0.6 0.0 copy-start.1
  0.6 0.0 copy-start
  2.0 0.0 copy-done.1
  2.0 0.6 %copy.12.weights = f32[1,2,3,128]{3,2,1,0:T(4,128)} copy(f32[1,2,3,128]{3,1,2,0:T(2,128)S(1)} %copy-done.1) | data formatting | bytes 6144 | tf_op args[5]
  2.6 0.0 copy-done
  2.6 0.6 %copy.11.observed = f32[1,2,2,3,128]{4,3,2,1,0:T(4,128)} copy(f32[1,2,2,3,128]{4,2,3,1,0:T(2,128)S(1)} %copy-done) | data formatting | bytes 12288 | tf_op args[4]
  3.2 40.3 %inversion.1 = (f32[5,2,128]{2,1,0:T(2,128)}, f32[5,32,128]{2,1,0:T(8,128)}) custom-call(f32[1]{0:T(128)S(6)} %copy.15.omega, f32[1]{0:T(128)S(6)} %copy.16.step_length, f32[1,2,2,3,5,32,128]{6,5,4,3,2,1,0:T(8,128)} %sources.1, f32[5,32,128]{2,1,0:T(8,128)} %log_cond.1, s32[1,128]{1,0:T(1,128)} %bitcast.1, f32[1,2,2,3,128]{4,3,2,1,0:T(4,128)} %copy.11.observed, ...), custom_call_target="tpu_custom_call" | custom-call | tf_op jit(solution)/shard_map/inversion/pallas_call | solution.py:446
  43.4 1.3 %copy.17 = f32[5,2,128]{2,1,0:T(2,128)} copy(f32[5,2,128]{2,1,0:T(2,128)} %get-tuple-element.4) | data formatting | bytes 10240
  44.7 1.5 %copy.18 = f32[5,32,128]{2,1,0:T(8,128)} copy(f32[5,32,128]{2,1,0:T(8,128)} %get-tuple-element.5) | data formatting | bytes 163840
Async XLA Ops:
  0.6 1.3 %copy-start.1 = (f32[1,2,3,128]{3,1,2,0:T(2,128)S(1)}, f32[1,2,3,128]{3,1,2,0:T(2,128)}, u32[]{:S(2)}) copy-start(f32[1,2,3,128]{3,1,2,0:T(2,128)} %param.14) | copy-start | bytes 9220
  0.6 1.9 %copy-start = (f32[1,2,2,3,128]{4,2,3,1,0:T(2,128)S(1)}, f32[1,2,2,3,128]{4,2,3,1,0:T(2,128)}, u32[]{:S(2)}) copy-start(f32[1,2,2,3,128]{4,2,3,1,0:T(2,128)} %param.13) | copy-start | bytes 18436

commit v2 on v1

--- a/solution.py
+++ b/solution.py
@@ -31,17 +31,14 @@
     return jnp.sum(plane.reshape(-1, 8, plane.shape[-1]), axis=0)
 
 
-def three_parts(value):
+def two_parts(value):
     high = value.astype(jnp.bfloat16)
-    rest = value - high.astype(F32)
-    middle = rest.astype(jnp.bfloat16)
-    low = (rest - middle.astype(F32)).astype(jnp.bfloat16)
-    return high, middle, low
+    return high, (value - high.astype(F32)).astype(jnp.bfloat16)
 
 
 def selected(chooser, value):
     total = None
-    for part in three_parts(value):
+    for part in two_parts(value):
         product = jnp.dot(chooser, part, preferred_element_type=F32)
         total = product if total is None else total + product
     return total
@@ -72,7 +69,7 @@
                 (log_cond, log_all.at[s]),
                 (receivers, rec_all.at[s]),
                 (observed.at[0, pol], obs_all.at[s]),
-                (weights.at[0, pol], wgt_all.at[s]),
+                (weights.at[0], wgt_all.at[s]),
                 (prior_grad, pg_parts.at[f]),
                 (prior_dir, pd_parts.at[f]),
             ]
@@ -115,7 +112,7 @@
             to_slab(1, j, log_cond, log_all.at[s]),
             to_slab(2, j, receivers, rec_all.at[s]),
             to_slab(3, j, observed.at[0, theirs], obs_all.at[s]),
-            to_slab(4, j, weights.at[0, theirs], wgt_all.at[s]),
+            to_slab(4, j, weights.at[0], wgt_all.at[s]),
         ]
 
     def freq_inputs(k):
@@ -172,6 +169,12 @@
             acc[1] + fold(u[0] * v[1] + u[1] * v[0]),
         )
 
+    def square_sum(acc, u):
+        return acc[0] + fold(u[0] * u[0] - u[1] * u[1]), acc[1] + fold(u[0] * u[1])
+
+    def square_totals(acc):
+        return whole_sum(acc[0]), 2.0 * whole_sum(acc[1])
+
     def totals(acc):
         return whole_sum(acc[0]), whole_sum(acc[1])
 
@@ -181,10 +184,10 @@
                 b = (residual[0, c, z], residual[1, c, z])
                 direction[c, z + 1, inner] = b[0]
                 direction[comps + c, z + 1, inner] = b[1]
-                acc = product_sum(acc, b, b)
+                acc = square_sum(acc, b)
             return acc
 
-        rho = totals(lax.fori_loop(0, nz, begin, (zero_acc, zero_acc)))
+        rho = square_totals(lax.fori_loop(0, nz, begin, (zero_acc, zero_acc), unroll=cz))
 
         def operate(z, acc):
             coup = coupling[z]
@@ -207,11 +210,11 @@
             return acc
 
         for iteration in range(ITERS):
-            curvature = totals(lax.fori_loop(0, nz, operate, (zero_acc, zero_acc)))
+            curvature = totals(lax.fori_loop(0, nz, operate, (zero_acc, zero_acc), unroll=cz))
             alpha = complex_div(rho, curvature)
             alpha = (jnp.broadcast_to(alpha[0], (ny, nx)), jnp.broadcast_to(alpha[1], (ny, nx)))
             if iteration + 1 == ITERS:
-                lax.fori_loop(0, nz, functools.partial(final, alpha), 0)
+                lax.fori_loop(0, nz, functools.partial(final, alpha), 0, unroll=cz)
                 break
 
             def update(z, acc, alpha=alpha, iteration=iteration):
@@ -229,10 +232,10 @@
                     )
                     residual[0, c, z] = left[0]
                     residual[1, c, z] = left[1]
-                    acc = product_sum(acc, left, left)
+                    acc = square_sum(acc, left)
                 return acc
 
-            rho_next = totals(lax.fori_loop(0, nz, update, (zero_acc, zero_acc)))
+            rho_next = square_totals(lax.fori_loop(0, nz, update, (zero_acc, zero_acc), unroll=cz))
             beta = complex_div(rho_next, rho)
             beta = (jnp.broadcast_to(beta[0], (ny, nx)), jnp.broadcast_to(beta[1], (ny, nx)))
             rho = rho_next
@@ -244,7 +247,7 @@
                     direction[comps + c, z + 1, inner] = residual[1, c, z] + (beta[0] * d[1] + beta[1] * d[0])
                 return carry
 
-            lax.fori_loop(0, nz, turn, 0)
+            lax.fori_loop(0, nz, turn, 0, unroll=cz)
 
     def stepped(target, alpha, z, c):
         d = (direction[c, z + 1, inner], direction[comps + c, z + 1, inner])
@@ -265,9 +268,11 @@
     recs = rec_all.shape[-1]
     for t in range(n_slab):
         layers = slice(t * cz, (t + 1) * cz)
-        small[0:comps] = obs_all[t, 0]
-        small[comps:2 * comps] = obs_all[t, 1]
-        small[2 * comps:3 * comps] = wgt_all[t]
+        for c in range(comps):
+            small[c:c + 1] = obs_all[t, c, 0:1]
+            small[comps + c:comps + c + 1] = obs_all[t, c, 1:2]
+            pair = wgt_all[t, c]
+            small[2 * comps + c:2 * comps + c + 1] = jnp.where(pol == 0, pair[0:1], pair[1:2])
         cell = rec_all[t]
         small[3 * comps:3 * comps + 1] = cell.astype(F32)
         columns = small[...].T
@@ -417,8 +422,8 @@
         vec(nz, ny, nx),
         vec(n_slab, cz, ny, nx),
         pltpu.VMEM((n_slab, 1, recs), jnp.int32),
-        vec(n_slab, 2, comps, recs),
-        vec(n_slab, comps, recs),
+        vec(n_slab, comps, 2, recs),
+        vec(n_slab, comps, POLS, recs),
         vec(16, recs),
         vec(nz, ny, nx),
         vec(cz, ny, nx),
@@ -443,7 +448,7 @@
         pltpu.SemaphoreType.DMA,
         pltpu.SemaphoreType.DMA,
     ]
-    return pl.pallas_call(
+    unit, trial = pl.pallas_call(
         functools.partial(kernel, (n_freq, n_slab, comps, cz, ny, nx)),
         out_shape=(
             jax.ShapeDtypeStruct(prior_grad.shape, F32),
@@ -456,7 +461,23 @@
             collective_id=0, has_side_effects=True, vmem_limit_bytes=56 * 1024 * 1024
         ),
         name="inversion",
-    )(omega, step, sources, log_cond, receivers.reshape(1, recs), observed, weights, prior_grad, prior_dir)
+    )(omega, step, sources, log_cond, receivers.reshape(1, recs), jnp.swapaxes(observed, 2, 3),
+      jnp.swapaxes(weights, 1, 2), prior_grad, prior_dir)
+    return pl.pallas_call(
+        hand_over,
+        out_shape=(
+            jax.ShapeDtypeStruct(unit.shape, F32),
+            jax.ShapeDtypeStruct(trial.shape, F32),
+        ),
+        in_specs=[inside, inside],
+        out_specs=(inside, inside),
+        name="hand_over",
+    )(unit, trial)
+
+
+def hand_over(unit, trial, unit_out, trial_out):
+    unit_out[...] = unit[...]
+    trial_out[...] = trial[...]
 
 
 def solution(mesh):

time: 46.5 us -> 38.1 us (0.82)
  Pallas kernels: 40.3 us -> 36 us
  local copies, waits for them, and re-layouts: 4.01 us -> 0 us
    pallas_call x1, Pallas kernels: 40.3 us -> 34.4 us  [per_device(): pl.pallas_call(functools.partial(kernel, (n_freq, n_slab, comps, cz, ny,...]
    unnamed x8 -> x0, local copies, waits for them, and re-layouts: 4.01 us -> none
    pallas_call x0 -> x1, Pallas kernels: none -> 1.55 us  [per_device(): pl.pallas_call(hand_over, out_shape=(jax.ShapeDtypeStruct(unit.shape, F32...]
where the time goes in v2:
time: 38.1 us; the launch traced here: 37.9 us
  Pallas kernels  36 us (94%)
  between operations  1.93 us (5%)
    pallas_call x1, Pallas kernels, per_device(): pl.pallas_call(functools.partial(kernel, (n_freq, n_slab, comps, cz, ny,...  34.4 us
    pallas_call x1, Pallas kernels, per_device(): pl.pallas_call(hand_over, out_shape=(jax.ShapeDtypeStruct(unit.shape, F32...  1.55 us

profile of v2, /device:TPU:0, one launch (start us, length us, event | category | flops | bytes accessed | tf_op | source)
XLA Modules:
  0.0 37.9 jit_solution(11940337188214297517)
XLA Ops:
  1.9 34.4 %inversion.1 = (f32[5,2,128]{2,1,0:T(2,128)}, f32[5,32,128]{2,1,0:T(8,128)}) custom-call(f32[1]{0:T(128)S(6)} %copy.11.omega, f32[1]{0:T(128)S(6)} %copy.12.step_length, f32[1,2,2,3,5,32,128]{6,5,4,3,2,1,0:T(8,128)} %sources.1, f32[5,32,128]{2,1,0:T(8,128)} %log_cond.1, s32[1,128]{1,0:T(1,128)} %bitcast.5, f32[1,2,3,2,128]{4,3,2,1,0:T(2,128)} %bitcast.3, ...), custom_call_target="tpu_custom_call" | custom-call | tf_op jit(solution)/shard_map/inversion/pallas_call | solution.py:451
  36.4 1.5 %hand_over.1 = (f32[5,2,128]{2,1,0:T(2,128)}, f32[5,32,128]{2,1,0:T(8,128)}) custom-call(f32[5,2,128]{2,1,0:T(2,128)} %get-tuple-element.4.unit, f32[5,32,128]{2,1,0:T(8,128)} %get-tuple-element.5.trial), custom_call_target="tpu_custom_call" | custom-call | tf_op jit(solution)/shard_map/hand_over/pallas_call | solution.py:466

commit v3 on v2

--- a/solution.py
+++ b/solution.py
@@ -44,14 +44,53 @@
     return total
 
 
+def exchange(
+    n_slab,
+    sources, log_cond, receivers, observed, weights,
+    sources_in, log_in, rec_in, obs_in, wgt_in,
+    send, recv,
+):
+    s = lax.axis_index("slab")
+    barrier = pltpu.get_barrier_semaphore()
+
+    def peer(j):
+        return {"slab": lax.rem(s + j, n_slab)}
+
+    for j in range(1, n_slab):
+        pl.semaphore_signal(barrier, inc=1, device_id=peer(j), device_id_type=pl.DeviceIdType.MESH)
+    pl.semaphore_wait(barrier, n_slab - 1)
+    copies = []
+    for j in range(1, n_slab):
+        theirs = lax.rem(lax.rem(s + j, n_slab), POLS)
+        moves = [
+            (sources.at[0, theirs], sources_in.at[j - 1]),
+            (log_cond, log_in.at[j - 1]),
+            (receivers, rec_in.at[j - 1]),
+            (observed.at[0, theirs], obs_in.at[j - 1]),
+            (weights.at[0], wgt_in.at[j - 1]),
+        ]
+        for i, (source, target) in enumerate(moves):
+            copies.append(
+                pltpu.make_async_remote_copy(
+                    src_ref=source, dst_ref=target, send_sem=send.at[i, j], recv_sem=recv.at[i, j],
+                    device_id=peer(j), device_id_type=pl.DeviceIdType.MESH,
+                )
+            )
+    for copy in copies:
+        copy.start()
+    for copy in copies:
+        copy.wait()
+
+
 def kernel(
     sizes,
     omega, step_length, sources, log_cond, receivers, observed, weights, prior_grad, prior_dir,
+    sources_in, log_in, rec_in, obs_in, wgt_in,
     unit_out, trial_out,
     residual, direction, image, field, adjoint, coupling, log_all, rec_all, obs_all, wgt_all,
     small, term, term_in, flat, outgoing, incoming, own_part, gathered, grad, pg_parts, pd_parts,
     pg_whole, pd_whole, sums_own, sums_in, unit_whole,
-    local_sem, slab_send, slab_recv, freq_send, freq_recv, pair_send, pair_recv,
+    local_sem, near_sem, slab_send, slab_recv, freq_send, freq_recv, pair_send, pair_recv,
 ):
     n_freq, n_slab, comps, cz, ny, nx = sizes
     nz, rows = cz * n_slab, cz * ny
@@ -75,6 +114,17 @@
             ]
         )
     ]
+    for j in range(1, n_slab):
+        t = lax.rem(s + n_slab - j, n_slab)
+        moves = [
+            (sources_in.at[j - 1], residual.at[:, :, pl.ds(t * cz, cz)]),
+            (log_in.at[j - 1], log_all.at[t]),
+            (rec_in.at[j - 1], rec_all.at[t]),
+            (obs_in.at[j - 1], obs_all.at[t]),
+            (wgt_in.at[j - 1], wgt_all.at[t]),
+        ]
+        for i, (a, b) in enumerate(moves):
+            local.append(pltpu.make_async_copy(a, b, near_sem.at[i, j]))
     for copy in local:
         copy.start()
 
@@ -91,10 +141,10 @@
     lax.fori_loop(1, n_freq, greet_freq, 0)
     lax.fori_loop(1, n_slab, greet_slab, 0)
 
-    def to_slab(i, j, source, target):
+    def to_slab(j, source, target):
         return pltpu.make_async_remote_copy(
             src_ref=source, dst_ref=target,
-            send_sem=slab_send.at[i, j], recv_sem=slab_recv.at[i, j],
+            send_sem=slab_send.at[j], recv_sem=slab_recv.at[j],
             device_id={"slab": lax.rem(s + j, n_slab)}, device_id_type=pl.DeviceIdType.MESH,
         )
 
@@ -105,16 +155,6 @@
             device_id={"freq": lax.rem(f + k, n_freq)}, device_id_type=pl.DeviceIdType.MESH,
         )
 
-    def slab_inputs(j):
-        theirs = lax.rem(lax.rem(s + j, n_slab), POLS)
-        return [
-            to_slab(0, j, sources.at[0, theirs], residual.at[:, :, own_layers]),
-            to_slab(1, j, log_cond, log_all.at[s]),
-            to_slab(2, j, receivers, rec_all.at[s]),
-            to_slab(3, j, observed.at[0, theirs], obs_all.at[s]),
-            to_slab(4, j, weights.at[0], wgt_all.at[s]),
-        ]
-
     def freq_inputs(k):
         return [
             to_freq(0, k, prior_grad, pg_parts.at[f]),
@@ -135,22 +175,8 @@
 
     lax.fori_loop(1, nz + 1, clear, 0)
 
-    pl.semaphore_wait(barrier, n_freq - 1 + n_slab - 1)
-    for j in range(1, n_slab):
-        for copy in slab_inputs(j):
-            copy.start()
-
-    def start_freq(k, carry):
-        for copy in freq_inputs(k):
-            copy.start()
-        return carry
-
-    lax.fori_loop(1, n_freq, start_freq, 0)
     for copy in local:
         copy.wait()
-    for j in range(1, n_slab):
-        for copy in slab_inputs(j):
-            copy.wait()
 
     def couple(t, carry):
         coupling[pl.ds(t * cz, cz)] = omega[0] * jnp.exp(log_all[t])
@@ -264,6 +290,15 @@
         return carry
 
     krylov_solve(field, keep_field)
+
+    pl.semaphore_wait(barrier, n_freq - 1 + n_slab - 1)
+
+    def start_freq(k, carry):
+        for copy in freq_inputs(k):
+            copy.start()
+        return carry
+
+    lax.fori_loop(1, n_freq, start_freq, 0)
 
     recs = rec_all.shape[-1]
     for t in range(n_slab):
@@ -376,9 +411,9 @@
     for i, (u, v) in enumerate(pairs):
         sums_own[i:i + 1] = jnp.sum(fold(u * v), axis=0, keepdims=True)
     for j in range(1, n_slab):
-        to_slab(5, j, sums_own, sums_in.at[j]).start()
+        to_slab(j, sums_own, sums_in.at[j]).start()
     for j in range(1, n_slab):
-        to_slab(5, j, sums_own, sums_in.at[j]).wait()
+        to_slab(j, sums_own, sums_in.at[j]).wait()
     sums = sums_own[...]
     for j in range(1, n_slab):
         sums = sums + sums_in[j]
@@ -441,28 +476,42 @@
         vec(n_slab, 8, nx),
         vec(cz, ny, nx),
         dma(7),
-        dma(6, n_slab),
-        dma(6, n_slab),
+        dma(5, n_slab),
+        dma(n_slab),
+        dma(n_slab),
         dma(4, n_freq),
         dma(4, n_freq),
         pltpu.SemaphoreType.DMA,
         pltpu.SemaphoreType.DMA,
     ]
+    local = (sources, log_cond, receivers.reshape(1, recs), jnp.swapaxes(observed, 2, 3), jnp.swapaxes(weights, 1, 2))
+    others = n_slab - 1
+    arrived = [(2, comps, cz, ny, nx), (cz, ny, nx), (1, recs), (comps, 2, recs), (comps, POLS, recs)]
+    far = pl.pallas_call(
+        functools.partial(exchange, n_slab),
+        out_shape=[
+            jax.ShapeDtypeStruct((others, *shape), value.dtype) for shape, value in zip(arrived, local)
+        ],
+        in_specs=[anywhere] * 5,
+        out_specs=[anywhere] * 5,
+        scratch_shapes=[dma(5, n_slab), dma(5, n_slab)],
+        compiler_params=pltpu.CompilerParams(collective_id=1, has_side_effects=True),
+        name="exchange",
+    )(*local)
     unit, trial = pl.pallas_call(
         functools.partial(kernel, (n_freq, n_slab, comps, cz, ny, nx)),
         out_shape=(
             jax.ShapeDtypeStruct(prior_grad.shape, F32),
             jax.ShapeDtypeStruct(log_cond.shape, F32),
         ),
-        in_specs=[smem, smem] + [anywhere] * 7,
+        in_specs=[smem, smem] + [anywhere] * 12,
         out_specs=(inside, inside),
         scratch_shapes=scratch,
         compiler_params=pltpu.CompilerParams(
             collective_id=0, has_side_effects=True, vmem_limit_bytes=56 * 1024 * 1024
         ),
         name="inversion",
-    )(omega, step, sources, log_cond, receivers.reshape(1, recs), jnp.swapaxes(observed, 2, 3),
-      jnp.swapaxes(weights, 1, 2), prior_grad, prior_dir)
+    )(omega, step, *local, prior_grad, prior_dir, *far)
     return pl.pallas_call(
         hand_over,
         out_shape=(

time: 38.1 us -> 35.4 us (0.929)
  Pallas kernels: 36 us -> 33.2 us
    pallas_call x1, Pallas kernels: 34.4 us -> 29 us  [per_device(): pl.pallas_call(functools.partial(kernel, (n_freq, n_slab, comps, cz, ny,...]
    pallas_call x0 -> x1, Pallas kernels: none -> 2.65 us  [per_device(): pl.pallas_call(functools.partial(exchange, n_slab), out_shape=[jax.ShapeD...]
where the time goes in v3:
time: 35.4 us; the launch traced here: 35.2 us
  Pallas kernels  33.2 us (94%)
  between operations  1.94 us (5%)
    pallas_call x1, Pallas kernels, per_device(): pl.pallas_call(functools.partial(kernel, (n_freq, n_slab, comps, cz, ny,...  29 us
    pallas_call x1, Pallas kernels, per_device(): pl.pallas_call(functools.partial(exchange, n_slab), out_shape=[jax.ShapeD...  2.65 us
    pallas_call x1, Pallas kernels, per_device(): pl.pallas_call(hand_over, out_shape=(jax.ShapeDtypeStruct(unit.shape, F32...  1.55 us

profile of v3, /device:TPU:0, one launch (start us, length us, event | category | flops | bytes accessed | tf_op | source)
XLA Modules:
  0.0 35.2 jit_solution(4825191327438184829)
XLA Ops:
  1.9 2.6 %exchange.1 = (f32[1,2,3,5,32,128]{5,4,3,2,1,0:T(8,128)}, f32[1,5,32,128]{3,2,1,0:T(8,128)}, s32[1,1,128]{2,1,0:T(1,128)}, f32[1,3,2,128]{3,2,1,0:T(2,128)}, f32[1,3,2,128]{3,2,1,0:T(2,128)}) custom-call(f32[1,2,2,3,5,32,128]{6,5,4,3,2,1,0:T(8,128)} %sources.3, f32[5,32,128]{2,1,0:T(8,128)} %log_cond.3, s32[1,128]{1,0:T(1,128)} %bitcast.7, ...), custom_call_target="tpu_custom_call" | custom-call | tf_op jit(solution)/shard_map/exchange/pallas_call | solution.py:490
  4.6 29.0 %inversion.1 = (f32[5,2,128]{2,1,0:T(2,128)}, f32[5,32,128]{2,1,0:T(8,128)}) custom-call(f32[1]{0:T(128)S(6)} %copy.11.omega, f32[1]{0:T(128)S(6)} %copy.12.step_length, f32[1,2,2,3,5,32,128]{6,5,4,3,2,1,0:T(8,128)} %sources.3, f32[5,32,128]{2,1,0:T(8,128)} %log_cond.3, s32[1,128]{1,0:T(1,128)} %bitcast.8, f32[1,2,3,2,128]{4,3,2,1,0:T(2,128)} %bitcast.4, ...), custom_call_target="tpu_custom_call" | custom-call | tf_op jit(solution)/shard_map/inversion/pallas_call | solution.py:501
  33.6 1.5 %hand_over.1 = (f32[5,2,128]{2,1,0:T(2,128)}, f32[5,32,128]{2,1,0:T(8,128)}) custom-call(f32[5,2,128]{2,1,0:T(2,128)} %get-tuple-element.14.unit, f32[5,32,128]{2,1,0:T(8,128)} %get-tuple-element.15.trial), custom_call_target="tpu_custom_call" | custom-call | tf_op jit(solution)/shard_map/hand_over/pallas_call | solution.py:515
